TPU v7x, 128 devices: a whole 4x4x4 slice. The times are simulated.
128 devices in a mesh: data: 1, hid: 16 (over z, y), vocab: 8 (over x, core).
Axes of the slice: x: 4, y: 4, z: 4, core: 2. Of those that a mesh axis runs over, the one named last changes fastest.
Arguments:
- h_states: bfloat16 [1024, 4096], P('data', 'hid')
- w_head: bfloat16 [4096, 32768], P('hid', 'vocab')
- inv_temp: float32 [1024], P('data')
- tgt_ids: int32 [1024], P('data')
Outputs:
- output 1: float32 [1024, 32768], P('data', ('vocab', 'hid'))
- output 2: float32 [1024], P('data')
All inputs are finite; a program needn't handle non-finite values.
Results may differ from a plain program's by a relative error of at most 0.001.
Values are sent between devices in bfloat16 or wider.
A program may use at most 1 GiB of HBM per device.

v0:
```python
import jax
import jax.numpy as jnp
from jax import lax
from jax.sharding import PartitionSpec as P


def solution(mesh):
    hid_size = mesh.shape["hid"]
    voc_size = mesh.shape["vocab"]

    def local_step(h_blk, w_blk, temp_blk, tgt_blk):
        part_logits = jnp.dot(h_blk, w_blk, preferred_element_type=jnp.float32)
        logits = lax.psum_scatter(part_logits, "hid", scatter_dimension=1, tiled=True) * temp_blk[:, None]
        local_cols = logits.shape[1]
        glob_max = lax.pmax(jnp.max(logits, axis=1), ("vocab", "hid"))
        exp_vals = jnp.exp(logits - glob_max[:, None])
        glob_sum = lax.psum(jnp.sum(exp_vals, axis=1), ("vocab", "hid"))
        local_cdf = jnp.cumsum(exp_vals / glob_sum[:, None], axis=1)
        hid_tots = lax.all_gather(local_cdf[:, -1], "hid")
        vocab_tots = lax.all_gather(jnp.sum(hid_tots, axis=0), "vocab")
        hid_idx = lax.axis_index("hid")
        voc_idx = lax.axis_index("vocab")
        hid_off = jnp.sum(jnp.where((jnp.arange(hid_size) < hid_idx)[:, None], hid_tots, 0.0), axis=0)
        voc_off = jnp.sum(jnp.where((jnp.arange(voc_size) < voc_idx)[:, None], vocab_tots, 0.0), axis=0)
        cdf_blk = local_cdf + (voc_off + hid_off)[:, None]
        col_start = (voc_idx * hid_size + hid_idx) * local_cols
        local_pos = tgt_blk - col_start
        in_range = (local_pos >= 0) & (local_pos < local_cols)
        picked = jnp.take_along_axis(cdf_blk, jnp.clip(local_pos, 0, local_cols - 1)[:, None], axis=1)[:, 0]
        cdf_tgt = lax.psum(jnp.where(in_range, picked, 0.0), ("vocab", "hid"))
        return cdf_blk, cdf_tgt

    return jax.shard_map(local_step, mesh=mesh, in_specs=(P("data", "hid"), P("hid", "vocab"), P("data"), P("data")), out_specs=(P("data", ("vocab", "hid")), P("data")), check_vma=False)
```

profile of v0, /device:TPU:1, one launch (start us, length us, event | category | flops | bytes accessed | tf_op | source)
XLA Modules:
  0.0 389.6 jit_solution(9978760256249286440)
XLA Ops:
  7.2 1.5 copy-done
  8.8 9.1 %fusion.6 = f32[1024,4096]{1,0:T(8,128)} fusion(bf16[1024,256]{1,0:T(8,128)(2,1)} %param.4, bf16[256,4096]{1,0:T(8,128)(2,1)S(1)} %copy-done), kind=kOutput, calls=%fused_computation.21 | convolution fusion | flops 2147483648 | bytes 19398656 | tf_op jit(solution)/shard_map/dot_general | solution.py:12
  17.9 0.6 copy-done.4
  18.6 112.7 %reduce-scatter.2.cloned.1.call-done = f32[1024,256]{1,0:T(8,128)} async-done(((f32[1024,4096]{1,0:T(8,128)}), f32[1024,256]{1,0:T(8,128)}) %reduce-scatter.2.cloned.1.call-update) | async-done | bytes 1048592 | tf_op jit(solution)/shard_map/reduce_scatter | solution.py:13
  131.3 1.7 multiply_reduce_fusion
  133.0 65.1 %pmax.7 = f32[1024]{0:T(1024)S(1)} all-reduce(f32[1024]{0:T(1024)S(1)} %multiply_reduce_fusion), channel_id=1, replica_groups=mesh['data'=1,'hid'=16,'vocab'=8] {'vocab','hid'}, use_global_device_ids=true, to_apply=%region_2.0 | all-reduce | flops 1024 | bytes 8192 | tf_op jit(solution)/shard_map/pmax | solution.py:15
  198.1 1.7 fusion.1
  199.8 64.1 %psum.14 = f32[1024]{0:T(1024)S(1)} all-reduce(f32[1024]{0:T(1024)S(1)} %fusion.1), channel_id=1, replica_groups=mesh['data'=1,'hid'=16,'vocab'=8] {'vocab','hid'}, use_global_device_ids=true, to_apply=%region_4.0 | all-reduce | flops 1024 | bytes 8192 | tf_op jit(solution)/shard_map/psum | solution.py:17
  263.9 1.4 fusion
  265.4 1.7 reshape.52
  267.1 2.2 copy.13
  269.3 1.6 fusion.5
  271.0 0.1 broadcast_add_fusion.1
  271.0 0.3 copy.14
  271.4 1.3 copy.15
  272.7 15.7 %all-gather = f32[16384,1]{0,1:T(1,128)S(1)} all-gather(f32[1024,1]{0,1:T(1,128)S(1)} %slice.16), channel_id=2, replica_groups=mesh['data'=1,'hid'=16,'vocab'=8] {'hid'}, dimensions={0}, use_global_device_ids=true | all-gather | bytes 69632 | tf_op jit(solution)/shard_map/all_gather | solution.py:19
  288.4 0.5 broadcast.52
  288.9 0.8 reduce.3
  289.8 0.1 select_reduce_fusion
  289.9 18.6 %all-gather.1 = f32[8192]{0:T(1024)S(1)} all-gather(f32[1024]{0:T(1024)S(1)} %get-tuple-element.3), channel_id=3, replica_groups=mesh['data'=1,'hid'=16,'vocab'=8] {'vocab'}, dimensions={0}, use_global_device_ids=true | all-gather | bytes 36864 | tf_op jit(solution)/shard_map/all_gather | solution.py:20
  308.5 0.1 select_reduce_fusion.1
  308.6 1.4 broadcast_add_fusion
  310.1 8.6 %gather_fusion = f32[1024]{0:T(1024)S(1)} fusion(f32[1024,256]{1,0:T(8,128)S(1)} %broadcast_add_fusion, s32[1024]{0:T(1024)S(1)} %bitcast.14), kind=kCustom, calls=%fused_computation | custom fusion | bytes 16384 | tf_op jit(solution)/shard_map/jit(take_along_axis)/gather | solution.py:29
  318.7 64.1 %psum.15 = f32[1024]{0:T(1024)} all-reduce(f32[1024]{0:T(1024)S(1)} %select_select_fusion), channel_id=1, replica_groups=mesh['data'=1,'hid'=16,'vocab'=8] {'vocab','hid'}, use_global_device_ids=true, to_apply=%region_10.11 | all-reduce | flops 1024 | bytes 8192 | tf_op jit(solution)/shard_map/psum | solution.py:30
  (25 shorter events, 0.3 us)
Async XLA Ops:
  7.2 1.6 copy-start
  7.2 124.1 %reduce-scatter.2.cloned.1.call-start = ((), (), s32[]{:S(2)}) async-start(), calls=%async_computation.1 | async-start | bytes 17825792 | tf_op jit(solution)/shard_map/reduce_scatter | solution.py:13
  17.9 0.7 copy-start.4
  17.9 113.4 %copy-start.3 = (f32[1024]{0:T(1024)S(1)}, f32[1024]{0:T(1024)}, u32[]{:S(2)}) copy-start(f32[1024]{0:T(1024)} %param.6) | copy-start | bytes 12292
  131.3 132.6 %copy-start.2 = (f32[1024,256]{1,0:T(8,128)S(1)}, f32[1024,256]{1,0:T(8,128)}, u32[]{:S(2)}) copy-start(f32[1024,256]{1,0:T(8,128)} %reduce-scatter.2.cloned.1.call-done) | copy-start | bytes 3145732
  310.1 8.6 %copy-start.1 = (f32[1024,256]{1,0:T(8,128)}, f32[1024,256]{1,0:T(8,128)S(1)}, u32[]{:S(2)}) copy-start(f32[1024,256]{1,0:T(8,128)S(1)} %broadcast_add_fusion) | copy-start | bytes 3145732
Sparse Core Ops, SparseCore 0:
  18.0 113.2 reduce-scatter.1
where the time goes:
time: 390 us
  blocking collectives  228 us (58%)
  waiting for transfers between devices  113 us (29%)
  local copies, waits for them, and re-layouts  16.9 us (4%)
  between operations  14.2 us (4%)
  matrix products  9.11 us (2%)
  other arithmetic  9.04 us (2%)
    reduce_scatter x1, waiting for transfers between devices, local_step(): lax.psum_scatter(part_logits, 'hid', scatter_dimension=1, tiled=True)  113 us
    pmax x1, blocking collectives, local_step(): glob_max = lax.pmax(jnp.max(logits, axis=1), ('vocab', 'hid'))  65.1 us
    psum x1, blocking collectives, local_step(): glob_sum = lax.psum(jnp.sum(exp_vals, axis=1), ('vocab', 'hid'))  64.1 us
    psum x1, blocking collectives, local_step(): cdf_tgt = lax.psum(jnp.where(in_range, picked, 0.0), ('vocab', 'hid'))  64.1 us
    all_gather x1, blocking collectives, local_step(): vocab_tots = lax.all_gather(jnp.sum(hid_tots, axis=0), 'vocab')  18.6 us
    all_gather x1, blocking collectives, local_step(): hid_tots = lax.all_gather(local_cdf[:, -1], 'hid')  15.7 us
    dot_general x1, matrix products, local_step(): part_logits = jnp.dot(h_blk, w_blk, preferred_element_type=jnp.float32)  9.11 us
    gather x1, local copies, waits for them, and re-layouts, local_step(): jnp.take_along_axis(cdf_blk, jnp.clip(local_pos, 0, local_cols - 1)[:, No...  8.59 us
  transfers between devices with their start and end apart: 1, of which 1 were waited for; matrix products, arithmetic and copies ran while one was open for 0% of the time, Pallas kernels for 0%

commit v1 on v0

v1 whole, which is shorter than its diff:
```python
import functools

import jax
import jax.numpy as jnp
from jax import lax
from jax.experimental import pallas as pl
from jax.experimental.pallas import tpu as pltpu
from jax.sharding import PartitionSpec as P

MESH = pl.DeviceIdType.MESH
BF = jnp.bfloat16
F32 = jnp.float32

B = 1024
KB = 256
TB = 256
PC = 64


def _mod4(a):
    return lax.rem(a, 4)


def _kernel(h_ref, w_ref, temp_ref, tgt_ref, cum_ref, so_ref, at_ref,
            H, Wsrc, Wv, cum, tcol, gcol, St, G1, S2, G2,
            loc, r1, r2, r3, rx, rxr, rd, rw, rs1, rs2, ss):
    hid = lax.axis_index("hid")
    voc = lax.axis_index("vocab")
    z, y, x, c = hid // 4, _mod4(hid), voc // 2, lax.rem(voc, 2)

    def dev(dz=0, dy=0, dx=0, dc=0):
        return {"hid": _mod4(z + dz) * 4 + _mod4(y + dy),
                "vocab": _mod4(x + dx) * 2 + lax.rem(c + dc, 2)}

    plane = [(a, b) for a in range(4) for b in range(4) if a or b]
    column = [(a, b) for a in range(4) for b in range(2) if a or b]

    barrier = pltpu.get_barrier_semaphore()
    for a, b in plane:
        pl.semaphore_signal(barrier, inc=1, device_id=dev(a, b), device_id_type=MESH)
    for a, b in column:
        pl.semaphore_signal(barrier, inc=1, device_id=dev(0, 0, a, b), device_id_type=MESH)

    own_h = pltpu.make_async_copy(h_ref, H.at[z, y], loc.at[0])
    own_h.start()
    all_w = pltpu.make_async_copy(w_ref, Wsrc, loc.at[1])
    all_w.start()
    own_w = pltpu.make_async_copy(
        w_ref.at[:, pl.ds(pl.multiple_of(hid * TB, TB), TB)],
        Wv.at[pl.ds(pl.multiple_of(hid * KB, KB), KB)], loc.at[2])
    own_w.start()

    for g in range(8):
        tcol[pl.ds(g * 128, 128), :] = jnp.broadcast_to(temp_ref[g:g + 1, :], (128, 128)).T
        gcol[pl.ds(g * 128, 128), :] = jnp.broadcast_to(tgt_ref[g:g + 1, :].astype(F32), (128, 128)).T

    pl.semaphore_wait(barrier, len(plane) + len(column))
    own_h.wait()

    def rows(p, dx=0, dc=0):
        return pl.ds(pl.multiple_of(_mod4(x + dx) * 256 + lax.rem(c + dc, 2) * 128 + p * PC, PC), PC)

    def single(p, f, s, dx=0, dc=0):
        dz, dy = (s, f) if p == 0 else (f, s)
        return H.at[_mod4(z + dz), _mod4(y + dy), rows(p, dx, dc), :]

    def group(p, s, dx=0, dc=0):
        if p == 0:
            return H.at[_mod4(z + s), :, rows(p, dx, dc), :]
        return H.at[:, _mod4(y + s), rows(p, dx, dc), :]

    def send(ref, to, recv_sem, cat):
        pltpu.make_async_remote_copy(src_ref=ref, dst_ref=ref, send_sem=ss.at[cat], recv_sem=recv_sem,
                                     device_id=to, device_id_type=MESH).start()

    def got(ref, sem):
        pltpu.make_async_copy(ref, ref, sem).wait()

    def first_dev(p, d):
        return dev(0, d) if p == 0 else dev(d, 0)

    def second_dev(p, d):
        return dev(d, 0) if p == 0 else dev(0, d)

    def send_w(a, b):
        peer = _mod4(z + a) * 4 + _mod4(y + b)
        pltpu.make_async_remote_copy(
            src_ref=Wsrc.at[:, pl.ds(pl.multiple_of(peer * TB, TB), TB)],
            dst_ref=Wv.at[pl.ds(pl.multiple_of(hid * KB, KB), KB)],
            send_sem=ss.at[3], recv_sem=rw.at[a * 4 + b], device_id=dev(a, b), device_id_type=MESH).start()

    def part(p, g, dx=0, dc=0):
        if g < 3:
            return single(p, (1, 3, 2)[g], 0, dx, dc)
        return group(p, (1, 3, 2)[g - 3], dx, dc)

    def to_partner(p, g, src):
        ref = part(p, g, src, 0)
        send(ref, dev(0, 0, 0, 1), rd.at[p, src, g], 2)

    def spread(p, g):
        ref = part(p, g)
        send(ref, dev(0, 0, 1), rx.at[p, 0, g], 1)
        send(ref, dev(0, 0, 3), rx.at[p, 1, g], 1)
        to_partner(p, g, 0)

    for p in range(2):
        me = single(p, 0, 0)
        for d in (1, 3, 2):
            send(me, first_dev(p, d), r1.at[p, d - 1], 0)
    for p in range(2):
        me = single(p, 0, 0)
        send(me, second_dev(p, 1), r2.at[p, 0, 0], 0)
        send(me, second_dev(p, 3), r2.at[p, 1, 0], 0)
    all_w.wait()
    order = [(0, 1), (0, 3), (1, 0), (3, 0), (1, 1), (3, 3), (1, 3), (3, 1),
             (0, 2), (2, 0), (1, 2), (2, 1), (3, 2), (2, 3), (2, 2)]
    for a, b in order[:4]:
        send_w(a, b)
    for i, d in enumerate((1, 3, 2)):
        for p in range(2):
            ref = single(p, d, 0)
            got(ref, r1.at[p, (4 - d) - 1])
            send(ref, second_dev(p, 1), r2.at[p, 0, d], 0)
            send(ref, second_dev(p, 3), r2.at[p, 1, d], 0)
            spread(p, i)
    for a, b in order[4:6]:
        send_w(a, b)
    for j in range(4):
        for p in range(2):
            for way, s in ((0, 3), (1, 1)):
                ref = single(p, j, s)
                got(ref, r2.at[p, way, j])
                if j % 2 == way:
                    send(ref, second_dev(p, 1 if way == 0 else 3), r3.at[p, j], 0)
    for p in range(2):
        spread(p, 3)
        spread(p, 4)
    for a, b in order[6:]:
        send_w(a, b)
    for p in range(2):
        for j in range(4):
            got(single(p, j, 2), r3.at[p, j])
        spread(p, 5)

    def from_x(g):
        for p in range(2):
            for way, dx in ((0, 3), (1, 1)):
                ref = part(p, g, dx)
                got(ref, rx.at[p, way, g])
                if p == way:
                    send(ref, dev(0, 0, 1 if way == 0 else 3), rxr.at[p, g], 1)
                to_partner(p, g, dx)

    def from_far(g):
        for p in range(2):
            got(part(p, g, 2), rxr.at[p, g])
            to_partner(p, g, 2)

    base = ((voc * 16 + hid) * TB).astype(F32)
    lane = lax.broadcasted_iota(jnp.int32, (128, 128), 1)
    col = lax.broadcasted_iota(jnp.int32, (256, TB), 1).astype(F32)
    tri = (lax.broadcasted_iota(jnp.int32, (TB, TB), 0) <= lax.broadcasted_iota(jnp.int32, (TB, TB), 1)).astype(F32).astype(BF)
    tri3 = jnp.concatenate([tri, tri, tri], axis=0)

    def compute(dx):
        for p in range(2):
            for g in range(6):
                got(part(p, g, dx, 1), rd.at[p, dx, g])
        q = _mod4(x + dx)
        rr = pl.ds(pl.multiple_of(q * 256, 256), 256)
        lhs = jnp.concatenate([H[k // 4, k % 4, rr, :] for k in range(16)], axis=1)
        zz = jnp.dot(lhs, Wv[...], preferred_element_type=F32)
        tc = tcol[rr, :]
        zz = zz * jnp.concatenate([tc, tc], axis=1)
        m = jnp.max(zz, axis=1, keepdims=True)
        e = jnp.exp(zz - m)
        e1 = e.astype(BF)
        f1 = e - e1.astype(F32)
        e2 = f1.astype(BF)
        e3 = (f1 - e2.astype(F32)).astype(BF)
        cs = jnp.dot(jnp.concatenate([e1, e2, e3], axis=1), tri3, preferred_element_type=F32)
        cum[rr, :] = cs
        gc = gcol[rr, :] - base
        t = jnp.sum(jnp.where(col <= jnp.concatenate([gc, gc], axis=1), e, 0.0), axis=1, keepdims=True)
        s = cs[:, TB - 1:TB]
        for i in range(2):
            a = slice(i * 128, (i + 1) * 128)
            pk = jnp.where(lane == 0, m[a], jnp.where(lane == 1, s[a], t[a])).T
            for k in range(3):
                St[k, pl.ds(q * 2 + i, 1), :] = pk[k:k + 1, :]
        pltpu.make_async_copy(cum.at[rr], cum_ref.at[rr], loc.at[3]).start()

    for g in range(6):
        from_x(g)
    own_w.wait()
    for a, b in plane:
        sender = _mod4(z + 4 - a) * 4 + _mod4(y + 4 - b)
        got(Wv.at[pl.ds(pl.multiple_of(sender * KB, KB), KB)], rw.at[a * 4 + b])
    compute(0)
    for g in range(3):
        from_far(g)
    compute(3)
    for g in range(3, 5):
        from_far(g)
    compute(1)
    from_far(5)
    compute(2)

    G1[hid] = St[...]
    for a, b in plane:
        pltpu.make_async_remote_copy(src_ref=St, dst_ref=G1.at[hid], send_sem=ss.at[4], recv_sem=rs1.at[a * 4 + b],
                                     device_id=dev(a, b), device_id_type=MESH).start()
    for a, b in plane:
        got(G1.at[_mod4(z + 4 - a) * 4 + _mod4(y + 4 - b)], rs1.at[a * 4 + b])
    mv = G1[0, 0]
    for k in range(1, 16):
        mv = jnp.maximum(mv, G1[k, 0])
    sv = jnp.zeros((8, 128), F32)
    pre = jnp.zeros((8, 128), F32)
    tv = jnp.zeros((8, 128), F32)
    for k in range(16):
        f = jnp.exp(G1[k, 0] - mv)
        sk = G1[k, 1] * f
        sv += sk
        tv += G1[k, 2] * f
        pre += jnp.where(k < hid, sk, 0.0)
    S2[0] = mv
    S2[1] = sv
    S2[2] = tv
    G2[voc] = S2[...]
    for a, b in column:
        pltpu.make_async_remote_copy(src_ref=S2, dst_ref=G2.at[voc], send_sem=ss.at[5], recv_sem=rs2.at[a * 2 + b],
                                     device_id=dev(0, 0, a, b), device_id_type=MESH).start()
    for a, b in column:
        got(G2.at[_mod4(x + 4 - a) * 2 + lax.rem(c + b, 2)], rs2.at[a * 2 + b])
    mx = G2[0, 0]
    for k in range(1, 8):
        mx = jnp.maximum(mx, G2[k, 0])
    tot = jnp.zeros((8, 128), F32)
    below = jnp.zeros((8, 128), F32)
    at = jnp.zeros((8, 128), F32)
    for k in range(8):
        f = jnp.exp(G2[k, 0] - mx)
        sk = G2[k, 1] * f
        tot += sk
        at += G2[k, 2] * f
        below += jnp.where(k < voc, sk, 0.0)
    so_ref[0] = jnp.exp(St[0] - mx) / tot
    so_ref[1] = (pre * jnp.exp(mv - mx) + below) / tot
    at_ref[...] = at / tot

    pltpu.make_async_copy(cum, cum_ref, loc.at[3]).wait()
    got(H.at[0:3, 0:4, 0:160, :], ss.at[0])
    got(H.at[0:3, 0:4, 0:480, :], ss.at[1])
    got(H.at[0:3, 0:4, 0:640, :], ss.at[2])
    got(Wv.at[0:15 * KB], ss.at[3])
    got(G1.at[0:15], ss.at[4])
    got(G2.at[0:7], ss.at[5])


def solution(mesh):
    dma = pltpu.SemaphoreType.DMA
    call = pl.pallas_call(
        _kernel,
        name="head_cdf",
        out_shape=(jax.ShapeDtypeStruct((B, TB), F32),
                   jax.ShapeDtypeStruct((2, 8, 128), F32),
                   jax.ShapeDtypeStruct((8, 128), F32)),
        in_specs=[pl.BlockSpec(memory_space=pl.ANY), pl.BlockSpec(memory_space=pl.ANY),
                  pl.BlockSpec(memory_space=pltpu.VMEM), pl.BlockSpec(memory_space=pltpu.VMEM)],
        out_specs=(pl.BlockSpec(memory_space=pl.ANY), pl.BlockSpec(memory_space=pltpu.VMEM),
                   pl.BlockSpec(memory_space=pltpu.VMEM)),
        scratch_shapes=[
            pltpu.VMEM((4, 4, B, KB), BF),
            pltpu.VMEM((KB, 4096), BF),
            pltpu.VMEM((4096, TB), BF),
            pltpu.VMEM((B, TB), F32),
            pltpu.VMEM((B, 128), F32),
            pltpu.VMEM((B, 128), F32),
            pltpu.VMEM((3, 8, 128), F32),
            pltpu.VMEM((16, 3, 8, 128), F32),
            pltpu.VMEM((3, 8, 128), F32),
            pltpu.VMEM((8, 3, 8, 128), F32),
            dma((5,)), dma((2, 3)), dma((2, 2, 4)), dma((2, 4)), dma((2, 2, 6)), dma((2, 6)), dma((2, 4, 6)),
            dma((16,)), dma((16,)), dma((8,)), dma((6,)),
        ],
        compiler_params=pltpu.CompilerParams(collective_id=0, has_side_effects=True, vmem_limit_bytes=48 * 2**20),
    )

    def local(h_blk, w_blk, temp, tgt):
        cum, so, at = call(h_blk, w_blk, temp.reshape(8, 128), tgt.reshape(8, 128))
        so = so.reshape(2, B)
        return cum * so[0][:, None] + so[1][:, None], at.reshape(B)

    return jax.shard_map(local, mesh=mesh,
                         in_specs=(P("data", "hid"), P("hid", "vocab"), P("data"), P("data")),
                         out_specs=(P("data", ("vocab", "hid")), P("data")), check_vma=False)
```

time: 390 us -> 68.3 us (0.18)
  blocking collectives: 228 us -> 0 us
  waiting for transfers between devices: 113 us -> 0 us
  Pallas kernels: 0 us -> 61.5 us
  between operations: 14.2 us -> 0.66 us
  local copies, waits for them, and re-layouts: 16.9 us -> 4.59 us
  matrix products: 9.11 us -> 0 us
  other arithmetic: 9.04 us -> 1.31 us
    psum x2 -> x0, blocking collectives: 128 us -> none  [the longest x1 64.1 us: local_step(): glob_sum = lax.psum(jnp.sum(exp_vals, axis=1), ('vocab', 'hid'))]
    reduce_scatter x1 -> x0, waiting for transfers between devices: 113 us -> none  [local_step(): lax.psum_scatter(part_logits, 'hid', scatter_dimension=1, tiled=True)]
    pmax x1 -> x0, blocking collectives: 65.1 us -> none  [local_step(): glob_max = lax.pmax(jnp.max(logits, axis=1), ('vocab', 'hid'))]
    pallas_call x0 -> x1, Pallas kernels: none -> 61.5 us  [local(): cum, so, at = call(h_blk, w_blk, temp.reshape(8, 128), tgt.reshape(8, 128))]
    all_gather x2 -> x0, blocking collectives: 34.4 us -> none  [the longest x1 18.6 us: local_step(): vocab_tots = lax.all_gather(jnp.sum(hid_tots, axis=0), 'vocab')]
    dot_general x1 -> x0, matrix products: 9.11 us -> none  [local_step(): part_logits = jnp.dot(h_blk, w_blk, preferred_element_type=jnp.float32)]
    gather x1 -> x0, local copies, waits for them, and re-layouts: 8.59 us -> none  [local_step(): jnp.take_along_axis(cdf_blk, jnp.clip(local_pos, 0, local_cols - 1)[:, No...]
    another operation x6 -> x0, local copies, waits for them, and re-layouts: 5.56 us -> none
  transfers between devices with their start and end apart: 1 -> 0, of which waited for: 1 -> 0; matrix products, arithmetic and copies ran while one was open for 0% -> 0% of each run, Pallas kernels for 0% -> 0%
where the time goes in v1:
time: 68.3 us; the launch traced here: 68.1 us
  Pallas kernels  61.5 us (90%)
  local copies, waits for them, and re-layouts  4.59 us (7%)
  other arithmetic  1.31 us (2%)
    pallas_call x1, Pallas kernels, local(): cum, so, at = call(h_blk, w_blk, temp.reshape(8, 128), tgt.reshape(8, 128))  61.5 us
    unnamed x9, local copies, waits for them, and re-layouts  4.59 us

profile of v1, /device:TPU:1, one launch (start us, length us, event | category | flops | bytes accessed | tf_op | source)
XLA Modules:
  0.0 68.1 jit_solution(228634531319565296)
XLA Ops:
  0.6 0.0 copy-start
  0.6 1.6 %copy-done = bf16[256,4096]{1,0:T(8,128)(2,1)S(1)} copy-done((bf16[256,4096]{1,0:T(8,128)(2,1)S(1)}, bf16[256,4096]{1,0:T(8,128)(2,1)}, u32[]{:S(2)}) %copy-start) | copy-done | bytes 2097176
  2.2 0.0 copy-start.1
  2.2 1.0 %copy-done.1 = bf16[1024,256]{1,0:T(8,128)(2,1)S(1)} copy-done((bf16[1024,256]{1,0:T(8,128)(2,1)S(1)}, bf16[1024,256]{1,0:T(8,128)(2,1)}, u32[]{:S(2)}) %copy-start.1) | copy-done | bytes 524312
  3.3 0.0 copy-start.2
  3.3 0.7 %copy-done.2 = f32[1024]{0:T(1024)S(1)} copy-done((f32[1024]{0:T(1024)S(1)}, f32[1024]{0:T(1024)}, u32[]{:S(2)}) %copy-start.2) | copy-done | bytes 4120
  4.0 0.0 copy-start.3
  4.0 0.7 %copy-done.3 = s32[1024]{0:T(1024)S(1)} copy-done((s32[1024]{0:T(1024)S(1)}, s32[1024]{0:T(1024)}, u32[]{:S(2)}) %copy-start.3) | copy-done | bytes 4120
  4.6 61.5 %head_cdf.1 = (f32[1024,256]{1,0:T(8,128)S(1)}, f32[2,8,128]{2,1,0:T(8,128)S(1)}, f32[8,128]{1,0:T(8,128)S(1)}) custom-call(bf16[1024,256]{1,0:T(8,128)(2,1)S(1)} %copy-done.1, bf16[256,4096]{1,0:T(8,128)(2,1)S(1)} %copy-done, f32[8,128]{1,0:T(8,128)S(1)} %bitcast.7, s32[8,128]{1,0:T(8,128)S(1)} %bitcast.8), custom_call_target="tpu_custom_call" | custom-call | tf_op jit(solution)/shard_map/head_cdf/pallas_call | solution.py:292
  66.1 1.3 %multiply_add_fusion = f32[1024,256]{1,0:T(8,128)} fusion(f32[1024,256]{1,0:T(8,128)S(1)} %get-tuple-element.5, f32[1024]{0:T(1024)S(1)} %get-tuple-element.9, f32[1024]{0:T(1024)S(1)} %get-tuple-element.8), kind=kLoop, calls=%fused_computation | loop fusion | flops 524288 | bytes 2105344 | tf_op jit(solution)/shard_map/add | solution.py:294
  67.5 0.6 copy.7
  (1 shorter events, 0.0 us)
Async XLA Ops:
  0.6 1.6 %copy-start = (bf16[256,4096]{1,0:T(8,128)(2,1)S(1)}, bf16[256,4096]{1,0:T(8,128)(2,1)}, u32[]{:S(2)}) copy-start(bf16[256,4096]{1,0:T(8,128)(2,1)} %w_ref.1) | copy-start | bytes 6291460
  2.2 1.0 %copy-start.1 = (bf16[1024,256]{1,0:T(8,128)(2,1)S(1)}, bf16[1024,256]{1,0:T(8,128)(2,1)}, u32[]{:S(2)}) copy-start(bf16[1024,256]{1,0:T(8,128)(2,1)} %h_ref.1) | copy-start | bytes 1572868
  3.3 0.7 %copy-start.2 = (f32[1024]{0:T(1024)S(1)}, f32[1024]{0:T(1024)}, u32[]{:S(2)}) copy-start(f32[1024]{0:T(1024)} %param.6) | copy-start | bytes 12292
  4.0 0.7 %copy-start.3 = (s32[1024]{0:T(1024)S(1)}, s32[1024]{0:T(1024)}, u32[]{:S(2)}) copy-start(s32[1024]{0:T(1024)} %param.7) | copy-start | bytes 12292
